TPU v7x, 32 devices: a whole 2x2x4 slice. The times are simulated.
32 devices in a mesh: trial: 4 (over y, x), rows: 2 (over core), cols: 4 (over z).
Axes of the slice: x: 2, y: 2, z: 4, core: 2. Of those that a mesh axis runs over, the one named last changes fastest.
Arguments:
- weight_gate: float32 [8192, 8192], P(('trial', 'rows'), 'cols'), parts along dimension 0, may hold values from -0.1875 to 0.1875
- moment_gate: float32 [8192, 8192], P(('trial', 'rows'), 'cols'), parts along dimension 0, may hold values from -6 to 6
- square_gate: float32 [8192, 8192], P(('trial', 'rows'), 'cols'), parts along dimension 0, may hold values from 0.1 to 10
- weight_up: float32 [8192, 8192], P(('trial', 'rows'), 'cols'), parts along dimension 0, may hold values from -0.1875 to 0.1875
- moment_up: float32 [8192, 8192], P(('trial', 'rows'), 'cols'), parts along dimension 0, may hold values from -6 to 6
- square_up: float32 [8192, 8192], P(('trial', 'rows'), 'cols'), parts along dimension 0, may hold values from 0.1 to 10
- norm_gain: float32 [8192], P(('trial', 'rows')), parts along dimension 0, may hold values from 0.25 to 1.75
Outputs:
- serving_gate: bfloat16 [8192, 8192], P('trial', 'cols'), parts along dimension 0
- serving_up: bfloat16 [8192, 8192], P('trial', 'cols'), parts along dimension 0
- column_gate: float32 [32768], P(('trial', 'cols')), parts along dimension 0
- column_up: float32 [32768], P(('trial', 'cols')), parts along dimension 0
There are 4 independent parts, one for each index of `trial`. A program takes and returns all parts, laid end to end along the dimension named above; each array names one. Nothing has to cross between parts.
All inputs are finite; a program needn't handle non-finite values. Where the computation divides by a largest or mean magnitude, that divisor is 1e-20 or more.
Results may differ from a plain program's by a relative error of at most 0.001.
Values may be sent and summed in bfloat16 or wider, within the bound.
A program may use at most 128 MiB of HBM per device.

v0:
```python
import jax
import jax.numpy as jnp
from jax import lax
from jax.sharding import PartitionSpec as P

D_MODEL = 2048


learn_rate = 0.02
decay_rate = 0.05
tiny_value = 1e-08


def shards(weight_gate, moment_gate, square_gate, weight_up, moment_up, square_up, norm_gain):
    whole_gate = weight_gate - learn_rate * (
        moment_gate / (jnp.sqrt(square_gate) + tiny_value) + decay_rate * weight_gate
    )
    whole_up = weight_up - learn_rate * (
        moment_up / (jnp.sqrt(square_up) + tiny_value) + decay_rate * weight_up
    )
    whole_gained_gate = whole_gate * norm_gain[:, None]
    whole_gained_up = whole_up * norm_gain[:, None]
    total_gate, total_up = lax.psum(
        (jnp.sum(jnp.abs(whole_gained_gate), axis=0), jnp.sum(jnp.abs(whole_gained_up), axis=0)),
        "rows",
    )
    column_gate = total_gate / D_MODEL
    column_up = total_up / D_MODEL
    narrow_gate, narrow_up = (
        (whole_gained_gate / column_gate).astype(jnp.bfloat16),
        (whole_gained_up / column_up).astype(jnp.bfloat16),
    )
    serving_gate, serving_up = (
        lax.all_gather(narrow_gate, "rows", axis=0, tiled=True),
        lax.all_gather(narrow_up, "rows", axis=0, tiled=True),
    )
    return (serving_gate, serving_up, column_gate, column_up)


def solution(mesh):
    return jax.shard_map(
        shards,
        mesh=mesh,
        in_specs=(
            P(("trial", "rows"), "cols"),
            P(("trial", "rows"), "cols"),
            P(("trial", "rows"), "cols"),
            P(("trial", "rows"), "cols"),
            P(("trial", "rows"), "cols"),
            P(("trial", "rows"), "cols"),
            P(("trial", "rows")),
        ),
        out_specs=(
            P("trial", "cols"),
            P("trial", "cols"),
            P(("trial", "cols")),
            P(("trial", "cols")),
        ),
        check_vma=False,
    )
```

profile of v0, /device:TPU:3, one launch (start us, length us, event | category | flops | bytes accessed | tf_op | source)
XLA Modules:
  0.0 111.3 jit_solution(3213533298670833020)
XLA Ops:
  7.2 0.0 all-gather.3.cloned.1.call-start
  7.2 25.5 %abs_reduce_fusion = (f32[2048]{0:T(1024)S(1)}, f32[1024,2048]{1,0:T(8,128)}, f32[2048]{0:T(1024)S(1)}, f32[1024,2048]{1,0:T(8,128)}) fusion(f32[1024]{0:T(1024)} %param.13, f32[1024,2048]{1,0:T(8,128)} %param.10, f32[1024,2048]{1,0:T(8,128)} %param.11, f32[1024,2048]{1,0:T(8,128)} %param.12, f32[1024,2048]{1,0:T(8,128)} %param.7, f32[1024,2048]{1,0:T(8,128)} %param.8, ...), kind=kLoop, calls=%fused_computation.1 | loop fusion | flops 37744640 | bytes 67129344 | tf_op jit(solution)/shard_map/reduce_sum | solution.py:24
  32.7 3.8 %all-reduce = (f32[2048]{0:T(1024)S(1)}, f32[2048]{0:T(1024)S(1)}) all-reduce(f32[2048]{0:T(1024)S(1)} %get-tuple-element.10, f32[2048]{0:T(1024)S(1)} %get-tuple-element.6), channel_id=1, replica_groups=mesh['trial'=4,'rows'=2,'cols'=4] {'rows'}, use_global_device_ids=true, to_apply=%region_1.0 | all-reduce | flops 4096 | bytes 32768 | tf_op jit(solution)/shard_map/psum | solution.py:23
  36.5 0.0 copy-start
  36.5 6.5 %divide_convert_fusion.1 = bf16[1024,2048]{1,0:T(8,128)(2,1)} fusion(f32[1024,2048]{1,0:T(8,128)} %get-tuple-element.11, f32[2048]{0:T(1024)S(1)} %broadcast_multiply_fusion.1), kind=kLoop, calls=%fused_computation.3 | loop fusion | flops 4194304 | bytes 12591104 | tf_op jit(solution)/shard_map/convert_element_type | solution.py:30
  43.0 0.0 all-gather.3.cloned.1.call-update
  43.0 0.0 copy-done
  43.0 0.0 all-gather.5.cloned.1.call-start
  43.1 0.0 copy-start.1
  43.1 6.6 %divide_convert_fusion = bf16[1024,2048]{1,0:T(8,128)(2,1)} fusion(f32[1024,2048]{1,0:T(8,128)} %get-tuple-element.7, f32[2048]{0:T(1024)S(1)} %broadcast_multiply_fusion), kind=kLoop, calls=%fused_computation | loop fusion | flops 4194304 | bytes 12591104 | tf_op jit(solution)/shard_map/convert_element_type | solution.py:31
  49.7 0.0 all-gather.5.cloned.1.call-update
  49.7 0.0 copy-done.1
  49.7 14.8 %all-gather.3.cloned.1.call-done = bf16[2048,2048]{1,0:T(8,128)(2,1)} async-done(((bf16[1024,2048]{1,0:T(8,128)(2,1)}), bf16[2048,2048]{1,0:T(8,128)(2,1)}) %all-gather.3.cloned.1.call-update) | async-done | bytes 8388624 | tf_op jit(solution)/shard_map/all_gather | solution.py:34
  64.4 23.2 %all-gather.5.cloned.1.call-done = bf16[2048,2048]{1,0:T(8,128)(2,1)} async-done(((bf16[1024,2048]{1,0:T(8,128)(2,1)}), bf16[2048,2048]{1,0:T(8,128)(2,1)}) %all-gather.5.cloned.1.call-update) | async-done | bytes 8388624 | tf_op jit(solution)/shard_map/all_gather | solution.py:35
  87.6 8.4 %copy.13 = bf16[2048,2048]{1,0:T(8,128)(2,1)} copy(bf16[2048,2048]{1,0:T(8,128)(2,1)} %all-gather.3.cloned.1.call-done) | data formatting | bytes 16777216
  96.1 8.4 %copy.14 = bf16[2048,2048]{1,0:T(8,128)(2,1)} copy(bf16[2048,2048]{1,0:T(8,128)(2,1)} %all-gather.5.cloned.1.call-done) | data formatting | bytes 16777216
  (2 shorter events, 0.0 us)
Async XLA Ops:
  7.2 57.3 %all-gather.3.cloned.1.call-start = ((), (), s32[]{:S(2)}) async-start(), calls=%async_computation | async-start | bytes 12582912 | tf_op jit(solution)/shard_map/all_gather | solution.py:34
  36.5 6.5 %copy-start = (f32[2048]{0:T(1024)}, f32[2048]{0:T(1024)S(1)}, u32[]{:S(2)}) copy-start(f32[2048]{0:T(1024)S(1)} %broadcast_multiply_fusion.1) | copy-start | bytes 24580
  43.0 44.6 %all-gather.5.cloned.1.call-start = ((), (), s32[]{:S(2)}) async-start(), calls=%async_computation.1 | async-start | bytes 12582912 | tf_op jit(solution)/shard_map/all_gather | solution.py:35
  43.1 6.6 %copy-start.1 = (f32[2048]{0:T(1024)}, f32[2048]{0:T(1024)S(1)}, u32[]{:S(2)}) copy-start(f32[2048]{0:T(1024)S(1)} %broadcast_multiply_fusion) | copy-start | bytes 24580
Sparse Core Ops, SparseCore 0:
  43.1 21.2 all-gather.2
  66.6 21.0 all-gather.4
where the time goes:
time: 112 us; the launch traced here: 111 us
  other arithmetic  38.5 us (34%)
  waiting for transfers between devices  38 us (34%)
  local copies, waits for them, and re-layouts  16.9 us (15%)
  between operations  14.1 us (13%)
  blocking collectives  3.79 us (3%)
    reduce_sum x1, other arithmetic, shards(): jnp.sum(jnp.abs(whole_gained_up), axis=0)  25.5 us
    all_gather x1, waiting for transfers between devices, shards(): lax.all_gather(narrow_up, 'rows', axis=0, tiled=True)  23.2 us
    unnamed x6, local copies, waits for them, and re-layouts  16.9 us
    all_gather x1, waiting for transfers between devices, shards(): lax.all_gather(narrow_gate, 'rows', axis=0, tiled=True)  14.8 us
    convert_element_type x1, other arithmetic, shards(): (whole_gained_up / column_up).astype(jnp.bfloat16)  6.57 us
    convert_element_type x1, other arithmetic, shards(): (whole_gained_gate / column_gate).astype(jnp.bfloat16)  6.49 us
    psum x1, blocking collectives, shards(): lax.psum((jnp.sum(jnp.abs(whole_gained_gate), axis=0), jnp.sum(jnp.abs(wh...  3.79 us
  transfers between devices with their start and end apart: 2, of which 2 were waited for; matrix products, arithmetic and copies ran while one was open for 6% of the time, Pallas kernels for 0%

commit v1 on v0

v1 whole, which is shorter than its diff:
```python
import functools

import jax
import jax.numpy as jnp
from jax import lax
from jax.experimental import pallas as pl
from jax.experimental.pallas import tpu as pltpu
from jax.sharding import PartitionSpec as P

learn_rate = 0.02
decay_rate = 0.05
tiny_value = 1e-08

LANES = 128
SLAB = 256
SLOTS = 8
MESH = pl.DeviceIdType.MESH


def exchange_kernel(
    n, wg, mg, sg, wu, mu, su, gain, out_g, out_u, col_g, col_u,
    w_buf, m_buf, s_buf, held, keep_scale, step_scale, parts,
    in_sem, part_send, part_recv, row_send, row_recv,
):
    rows, width = wg.shape
    slabs = width // SLAB
    steps = 2 * slabs
    chunk = min(rows, 256)
    me = lax.axis_index("rows")
    sources = ((wg, mg, sg), (wu, mu, su))
    outs = (out_g, out_u)
    cols = (col_g, col_u)
    buffers = (w_buf, m_buf, s_buf)

    def columns(j):
        return pl.ds(pl.multiple_of(j * SLAB, SLAB), SLAB)

    def loads(j, p):
        slot = lax.rem(2 * j + p, SLOTS)
        return [
            pltpu.make_async_copy(source.at[:, columns(j)], buffer.at[slot], in_sem.at[slot, i])
            for i, (source, buffer) in enumerate(zip(sources[p], buffers))
        ]

    def part_copy(j, p, k, owner):
        t = 2 * j + p
        return pltpu.make_async_remote_copy(
            src_ref=parts.at[t, owner],
            dst_ref=parts.at[t, owner],
            send_sem=part_send.at[t, k - 1],
            recv_sem=part_recv.at[t, k - 1],
            device_id={"rows": lax.rem(me + k, n)},
            device_id_type=MESH,
        )

    def row_copy(j, p, k, owner):
        t = 2 * j + p
        block = outs[p].at[pl.ds(pl.multiple_of(owner * rows, rows), rows), columns(j)]
        return pltpu.make_async_remote_copy(
            src_ref=block,
            dst_ref=block,
            send_sem=row_send.at[t, k - 1],
            recv_sem=row_recv.at[t, k - 1],
            device_id={"rows": lax.rem(me + k, n)},
            device_id_type=MESH,
        )

    def update(j, p):
        slot = lax.rem(2 * j + p, SLOTS)
        for copy in loads(j, p):
            copy.wait()

        def body(c, sums):
            at = pl.ds(pl.multiple_of(c * chunk, chunk), chunk)
            keep, scale = keep_scale[at, :], step_scale[at, :]
            new = []
            for i in range(SLAB // LANES):
                tile = pl.ds(i * LANES, LANES)
                square = s_buf[slot, at, tile]
                root = square * lax.rsqrt(square)
                value = w_buf[slot, at, tile] * keep - (m_buf[slot, at, tile] * scale) / (root + tiny_value)
                held[p, at, tile] = value
                new.append(sums[i] + jnp.sum(jnp.abs(value).reshape(chunk // 8, 8, LANES), axis=0))
            return tuple(new)

        zero = jnp.zeros((8, LANES), jnp.float32)
        sums = lax.fori_loop(0, rows // chunk, body, (zero,) * (SLAB // LANES))
        for i in range(SLAB // LANES):
            parts[2 * j + p, me, :, pl.ds(i * LANES, LANES)] = sums[i]

    def share_sums(j, p):
        for k in range(1, n):
            part_copy(j, p, k, me).start()

    def finish(j, p):
        t = 2 * j + p
        for k in range(1, n):
            part_copy(j, p, k, lax.rem(me + n - k, n)).wait_recv()
        total = parts[t, 0]
        for r in range(1, n):
            total = total + parts[t, r]
        column = jnp.sum(total, axis=0, keepdims=True) / (n * rows)
        cols[p][:, columns(j)] = column
        factor = 1.0 / column

        def body(c, carry):
            at = pl.ds(pl.multiple_of(c * chunk, chunk), chunk)
            to = pl.ds(pl.multiple_of(me * rows + c * chunk, chunk), chunk)
            outs[p][to, columns(j)] = (held[p, at, :] * factor).astype(jnp.bfloat16)
            return carry

        lax.fori_loop(0, rows // chunk, body, 0)

    def share_rows(j, p):
        for k in range(1, n):
            row_copy(j, p, k, me).start()

    ahead = min(SLOTS // 2, slabs)
    for j in range(ahead):
        for p in range(2):
            for copy in loads(j, p):
                copy.start()

    barrier = pltpu.get_barrier_semaphore()
    for k in range(1, n):
        pl.semaphore_signal(barrier, inc=1, device_id={"rows": lax.rem(me + k, n)}, device_id_type=MESH)

    for r in range(rows // LANES):
        spread = jnp.broadcast_to(gain[r : r + 1, :], (LANES, LANES)).T
        at = pl.ds(r * LANES, LANES)
        keep_scale[at, :] = spread * (1.0 - learn_rate * decay_rate)
        step_scale[at, :] = spread * learn_rate

    pl.semaphore_wait(barrier, n - 1)

    def refill(j, p):
        @pl.when(j + ahead < slabs)
        def _():
            for copy in loads(j + ahead, p):
                copy.start()

    def step(j, carry):
        update(j, 0)
        share_sums(j, 0)
        refill(j, 0)

        @pl.when(j > 0)
        def _():
            finish(j - 1, 1)
            share_rows(j - 1, 1)

        update(j, 1)
        share_sums(j, 1)
        refill(j, 1)
        finish(j, 0)
        share_rows(j, 0)
        return carry

    lax.fori_loop(0, slabs, step, 0)
    finish(slabs - 1, 1)
    share_rows(slabs - 1, 1)

    def drain(j, carry):
        for p in range(2):
            for k in range(1, n):
                part_copy(j, p, k, me).wait_send()
                row_copy(j, p, k, me).wait_send()
                row_copy(j, p, k, lax.rem(me + n - k, n)).wait_recv()
        return carry

    lax.fori_loop(0, slabs, drain, 0)


def store_kernel(pieces, gate, up, col_g, col_u, out_g, out_u, out_cg, out_cu, sem, col_sem):
    height = gate.shape[0] // pieces
    copies = []
    for p, (source, target) in enumerate(((gate, out_g), (up, out_u))):
        for i in range(pieces):
            at = pl.ds(i * height, height)
            copies.append(pltpu.make_async_copy(source.at[at, :], target.at[at, :], sem.at[p, i]))
    copies.append(pltpu.make_async_copy(col_g, out_cg, col_sem.at[0]))
    copies.append(pltpu.make_async_copy(col_u, out_cu, col_sem.at[1]))
    for copy in copies:
        copy.start()
    for copy in copies:
        copy.wait()


def solution(mesh):
    n = mesh.shape["rows"]

    def shards(weight_gate, moment_gate, square_gate, weight_up, moment_up, square_up, norm_gain):
        rows, width = weight_gate.shape
        steps = 2 * (width // SLAB)
        any_space = pl.BlockSpec(memory_space=pl.ANY)
        in_vmem = pl.BlockSpec(memory_space=pltpu.VMEM)
        shapes = (
            ((n * rows, width), jnp.bfloat16),
            ((n * rows, width), jnp.bfloat16),
            ((1, width), jnp.float32),
            ((1, width), jnp.float32),
        )
        dma = pltpu.SemaphoreType.DMA
        moved = pl.pallas_call(
            functools.partial(exchange_kernel, n),
            out_shape=tuple(pltpu.VMEM(*shape) for shape in shapes),
            in_specs=[any_space] * 6 + [in_vmem],
            out_specs=[in_vmem] * 4,
            scratch_shapes=[
                pltpu.VMEM((SLOTS, rows, SLAB), jnp.float32),
                pltpu.VMEM((SLOTS, rows, SLAB), jnp.float32),
                pltpu.VMEM((SLOTS, rows, SLAB), jnp.float32),
                pltpu.VMEM((2, rows, SLAB), jnp.float32),
                pltpu.VMEM((rows, LANES), jnp.float32),
                pltpu.VMEM((rows, LANES), jnp.float32),
                pltpu.VMEM((steps, n, 8, SLAB), jnp.float32),
                dma((SLOTS, 3)),
                dma((steps, max(n - 1, 1))),
                dma((steps, max(n - 1, 1))),
                dma((steps, max(n - 1, 1))),
                dma((steps, max(n - 1, 1))),
            ],
            compiler_params=pltpu.CompilerParams(
                collective_id=0, has_side_effects=True, vmem_limit_bytes=36 * 1024 * 1024
            ),
            name="exchange",
        )(
            weight_gate, moment_gate, square_gate, weight_up, moment_up, square_up,
            norm_gain.reshape(rows // LANES, LANES),
        )
        pieces = 4
        gate, up, col_g, col_u = pl.pallas_call(
            functools.partial(store_kernel, pieces),
            out_shape=tuple(jax.ShapeDtypeStruct(*shape) for shape in shapes),
            in_specs=[in_vmem] * 4,
            out_specs=[any_space] * 4,
            scratch_shapes=[dma((2, pieces)), dma((2,))],
            compiler_params=pltpu.CompilerParams(vmem_limit_bytes=1024 * 1024),
            name="store",
        )(*moved)
        return gate, up, col_g.reshape(width), col_u.reshape(width)

    held = P(("trial", "rows"), "cols")
    return jax.shard_map(
        shards,
        mesh=mesh,
        in_specs=(held,) * 6 + (P(("trial", "rows")),),
        out_specs=(P("trial", "cols"), P("trial", "cols"), P(("trial", "cols")), P(("trial", "cols"))),
        check_vma=False,
    )
```

time: 112 us -> 27.6 us (0.25)
  other arithmetic: 38.5 us -> 0 us
  waiting for transfers between devices: 38 us -> 0 us
  Pallas kernels: 0 us -> 26.1 us
  local copies, waits for them, and re-layouts: 16.9 us -> 0.68 us
  between operations: 14.1 us -> 0.65 us
  blocking collectives: 3.79 us -> 0 us
    all_gather x2 -> x0, waiting for transfers between devices: 37.9 us -> none  [the longest x1 23.2 us: shards(): lax.all_gather(narrow_up, 'rows', axis=0, tiled=True)]
    pallas_call x0 -> x2, Pallas kernels: none -> 26.1 us  [the longest x1 20.1 us: shards(): pl.pallas_call(functools.partial(exchange_kernel, n), out_shape=tuple((pl...]
    reduce_sum x1 -> x0, other arithmetic: 25.5 us -> none  [shards(): jnp.sum(jnp.abs(whole_gained_up), axis=0)]
    unnamed x6 -> x2, local copies, waits for them, and re-layouts: 16.9 us -> 0.68 us
    convert_element_type x2 -> x0, other arithmetic: 13.1 us -> none  [the longest x1 6.57 us: shards(): (whole_gained_up / column_up).astype(jnp.bfloat16)]
    psum x1 -> x0, blocking collectives: 3.79 us -> none  [shards(): lax.psum((jnp.sum(jnp.abs(whole_gained_gate), axis=0), jnp.sum(jnp.abs(wh...]
  transfers between devices with their start and end apart: 2 -> 0, of which waited for: 2 -> 0; matrix products, arithmetic and copies ran while one was open for 6% -> 0% of each run, Pallas kernels for 0% -> 0%
where the time goes in v1:
time: 27.6 us; the launch traced here: 27.4 us
  Pallas kernels  26.1 us (95%)
  local copies, waits for them, and re-layouts  0.68 us (2%)
  between operations  0.65 us (2%)
    pallas_call x1, Pallas kernels, shards(): pl.pallas_call(functools.partial(exchange_kernel, n), out_shape=tuple((pl...  20.1 us
    pallas_call x1, Pallas kernels, shards(): pl.pallas_call(functools.partial(store_kernel, pieces), out_shape=tuple((...  5.95 us
    unnamed x2, local copies, waits for them, and re-layouts  0.68 us

profile of v1, /device:TPU:3, one launch (start us, length us, event | category | flops | bytes accessed | tf_op | source)
XLA Modules:
  0.0 27.4 jit_solution(16764290825659072984)
XLA Ops:
  0.6 0.0 copy-start
  0.6 0.7 %copy-done = f32[1024]{0:T(1024)S(1)} copy-done((f32[1024]{0:T(1024)S(1)}, f32[1024]{0:T(1024)}, u32[]{:S(2)}) %copy-start) | copy-done | bytes 4120
  1.3 20.1 %exchange.1 = (bf16[2048,2048]{1,0:T(8,128)(2,1)S(1)}, bf16[2048,2048]{1,0:T(8,128)(2,1)S(1)}, f32[1,2048]{1,0:T(1,128)S(1)}, f32[1,2048]{1,0:T(1,128)S(1)}) custom-call(f32[1024,2048]{1,0:T(8,128)} %wg.1, f32[1024,2048]{1,0:T(8,128)} %mg.1, f32[1024,2048]{1,0:T(8,128)} %sg.1, f32[1024,2048]{1,0:T(8,128)} %wu.1, f32[1024,2048]{1,0:T(8,128)} %mu.1, ...), custom_call_target="tpu_custom_call" | custom-call | tf_op jit(solution)/shard_map/exchange/pallas_call | solution.py:204
  21.5 6.0 %store.1 = (bf16[2048,2048]{1,0:T(8,128)(2,1)}, bf16[2048,2048]{1,0:T(8,128)(2,1)}, f32[1,2048]{1,0:T(1,128)}, f32[1,2048]{1,0:T(1,128)}) custom-call(bf16[2048,2048]{1,0:T(8,128)(2,1)S(1)} %get-tuple-element.12.gate, bf16[2048,2048]{1,0:T(8,128)(2,1)S(1)} %get-tuple-element.13.up, f32[1,2048]{1,0:T(1,128)S(1)} %get-tuple-element.14.col_g, ...), custom_call_target="tpu_custom_call" | custom-call | tf_op jit(solution)/shard_map/store/pallas_call | solution.py:232
Async XLA Ops:
  0.6 0.7 %copy-start = (f32[1024]{0:T(1024)S(1)}, f32[1024]{0:T(1024)}, u32[]{:S(2)}) copy-start(f32[1024]{0:T(1024)} %param.13) | copy-start | bytes 12292

commit v2 on v1

--- a/solution.py
+++ b/solution.py
@@ -19,8 +19,8 @@
 
 def exchange_kernel(
     n, wg, mg, sg, wu, mu, su, gain, out_g, out_u, col_g, col_u,
-    w_buf, m_buf, s_buf, held, keep_scale, step_scale, parts,
-    in_sem, part_send, part_recv, row_send, row_recv,
+    w_buf, m_buf, s_buf, held, gain_buf, keep_scale, step_scale, parts,
+    gain_sem, in_sem, part_send, part_recv, row_send, row_recv,
 ):
     rows, width = wg.shape
     slabs = width // SLAB
@@ -115,6 +115,8 @@
         for k in range(1, n):
             row_copy(j, p, k, me).start()
 
+    gain_copy = pltpu.make_async_copy(gain, gain_buf, gain_sem)
+    gain_copy.start()
     ahead = min(SLOTS // 2, slabs)
     for j in range(ahead):
         for p in range(2):
@@ -125,8 +127,9 @@
     for k in range(1, n):
         pl.semaphore_signal(barrier, inc=1, device_id={"rows": lax.rem(me + k, n)}, device_id_type=MESH)
 
+    gain_copy.wait()
     for r in range(rows // LANES):
-        spread = jnp.broadcast_to(gain[r : r + 1, :], (LANES, LANES)).T
+        spread = jnp.broadcast_to(gain_buf[r : r + 1, :], (LANES, LANES)).T
         at = pl.ds(r * LANES, LANES)
         keep_scale[at, :] = spread * (1.0 - learn_rate * decay_rate)
         step_scale[at, :] = spread * learn_rate
@@ -204,16 +207,18 @@
         moved = pl.pallas_call(
             functools.partial(exchange_kernel, n),
             out_shape=tuple(pltpu.VMEM(*shape) for shape in shapes),
-            in_specs=[any_space] * 6 + [in_vmem],
+            in_specs=[any_space] * 7,
             out_specs=[in_vmem] * 4,
             scratch_shapes=[
                 pltpu.VMEM((SLOTS, rows, SLAB), jnp.float32),
                 pltpu.VMEM((SLOTS, rows, SLAB), jnp.float32),
                 pltpu.VMEM((SLOTS, rows, SLAB), jnp.float32),
                 pltpu.VMEM((2, rows, SLAB), jnp.float32),
+                pltpu.VMEM((rows // LANES, LANES), jnp.float32),
                 pltpu.VMEM((rows, LANES), jnp.float32),
                 pltpu.VMEM((rows, LANES), jnp.float32),
                 pltpu.VMEM((steps, n, 8, SLAB), jnp.float32),
+                dma,
                 dma((SLOTS, 3)),
                 dma((steps, max(n - 1, 1))),
                 dma((steps, max(n - 1, 1))),

time: 27.6 us -> 27.7 us (level)
  no operation moved by 1% of the time
where the time goes in v2:
time: 27.7 us; the launch traced here: 27.5 us
  Pallas kernels  26.2 us (95%)
  local copies, waits for them, and re-layouts  0.68 us (2%)
  between operations  0.65 us (2%)
    pallas_call x1, Pallas kernels, shards(): pl.pallas_call(functools.partial(exchange_kernel, n), out_shape=tuple((pl...  20.2 us
    pallas_call x1, Pallas kernels, shards(): pl.pallas_call(functools.partial(store_kernel, pieces), out_shape=tuple((...  5.95 us
    unnamed x2, local copies, waits for them, and re-layouts  0.68 us

profile of v2, /device:TPU:3, one launch (start us, length us, event | category | flops | bytes accessed | tf_op | source)
XLA Modules:
  0.0 27.5 jit_solution(590048044075191888)
XLA Ops:
  0.6 0.0 copy-start
  0.6 0.7 %copy-done = f32[1024]{0:T(1024)S(1)} copy-done((f32[1024]{0:T(1024)S(1)}, f32[1024]{0:T(1024)}, u32[]{:S(2)}) %copy-start) | copy-done | bytes 4120
  1.3 20.2 %exchange.1 = (bf16[2048,2048]{1,0:T(8,128)(2,1)S(1)}, bf16[2048,2048]{1,0:T(8,128)(2,1)S(1)}, f32[1,2048]{1,0:T(1,128)S(1)}, f32[1,2048]{1,0:T(1,128)S(1)}) custom-call(f32[1024,2048]{1,0:T(8,128)} %wg.1, f32[1024,2048]{1,0:T(8,128)} %mg.1, f32[1024,2048]{1,0:T(8,128)} %sg.1, f32[1024,2048]{1,0:T(8,128)} %wu.1, f32[1024,2048]{1,0:T(8,128)} %mu.1, ...), custom_call_target="tpu_custom_call" | custom-call | tf_op jit(solution)/shard_map/exchange/pallas_call | solution.py:207
  21.6 6.0 %store.1 = (bf16[2048,2048]{1,0:T(8,128)(2,1)}, bf16[2048,2048]{1,0:T(8,128)(2,1)}, f32[1,2048]{1,0:T(1,128)}, f32[1,2048]{1,0:T(1,128)}) custom-call(bf16[2048,2048]{1,0:T(8,128)(2,1)S(1)} %get-tuple-element.12.gate, bf16[2048,2048]{1,0:T(8,128)(2,1)S(1)} %get-tuple-element.13.up, f32[1,2048]{1,0:T(1,128)S(1)} %get-tuple-element.14.col_g, ...), custom_call_target="tpu_custom_call" | custom-call | tf_op jit(solution)/shard_map/store/pallas_call | solution.py:237
Async XLA Ops:
  0.6 0.7 %copy-start = (f32[1024]{0:T(1024)S(1)}, f32[1024]{0:T(1024)}, u32[]{:S(2)}) copy-start(f32[1024]{0:T(1024)} %param.13) | copy-start | bytes 12292
